TPU v7x, 32 devices: a whole 2x2x4 slice. The times are simulated.
32 devices in a mesh: dp: 2 (over core), expert: 4 (over y, x), mp: 4 (over z).
Axes of the slice: x: 2, y: 2, z: 4, core: 2. Of those that a mesh axis runs over, the one named last changes fastest.
Arguments:
- hidden: bfloat16 [3072, 2, 7168], P(('dp', 'expert'), None, 'mp'), may hold values from -6 to 6
- cotangent: bfloat16 [3072, 2048], P(('dp', 'expert'), 'mp'), may hold values from -6 to 6
- routes: int32 [3072, 2], P(('dp', 'expert')), may hold values from 0 to 3, all different within a row; in each aligned block of 384 rows (0 to 383, 384 to 767, ...) at most 288 rows name the same one
- combine: float32 [3072, 2], P(('dp', 'expert')), may hold values from 0.1 to 0.9
- block_pair: int32 [8, 12], P(('dp', 'expert')), may hold values from 0 to 11, each once within a row
- lengths: int32 [8, 12], P(('dp', 'expert')), may hold values from 4 to 32
- log_ratio: float32 [8, 12], P(('dp', 'expert')), may hold values from -30 to 30
Outputs:
- grad_down: float32 [4, 7168, 2048], P('expert', ('mp', 'dp'))
- expert_load: float32 [4], replicated
Inputs may be any that keep to these rules, and one draw needn't show every extreme that they name: `routes`: each row names 2 different experts; in each aligned block of 384 rows (the rows of one device) no expert is named more than 288 times, and in some blocks one expert is named exactly 288 times. `block_pair`: each row holds every number of 0 to 11 once; value v marks the chosen response of the row's pair v // 2 if v is even, its rejected response if v is odd.
All inputs are finite; a program needn't handle non-finite values.
Results may differ from a plain program's by a relative error of at most 0.0029.
Values may be sent and summed in bfloat16 or wider, within the bound.
A program may use at most 128 MiB of HBM per device.

v0:
```python
import jax
import jax.numpy as jnp
from jax import lax
from jax.sharding import PartitionSpec as P

EXP_DEV = 1
LEN = 32


beta_scale = 0.1


def token_weights(combine, block_pair, lengths, log_ratio, block_len):
    blocks = block_pair.shape[1]
    labels = jnp.arange(blocks, dtype=jnp.int32)
    matches = block_pair[:, :, None] == labels[None, None, :]
    by_label = jnp.sum(jnp.where(matches, log_ratio[:, :, None], 0.0), axis=1)
    margin = by_label[:, 0::2] - by_label[:, 1::2]
    pair_coef = beta_scale * jax.nn.sigmoid(-beta_scale * margin)
    owners = block_pair // 2
    pair_ids = jnp.arange(blocks // 2, dtype=jnp.int32)
    picked = owners[:, :, None] == pair_ids[None, None, :]
    block_coef = jnp.sum(jnp.where(picked, pair_coef[:, None, :], 0.0), axis=2)
    block_weight = jnp.where(block_pair % 2 == 0, -block_coef, block_coef)
    position = jnp.arange(block_len, dtype=jnp.int32)
    within = position[None, None, :] < lengths[:, :, None]
    per_token = jnp.where(within, block_weight[:, :, None], 0.0).reshape(-1)
    return (combine * per_token[:, None], within.reshape(-1))


def body(hidden, cotangent, routes, combine, block_pair, lengths, log_ratio):
    weight, within = token_weights(combine, block_pair, lengths, log_ratio, LEN)
    tok_rows = routes.shape[0]
    route_top = routes.shape[1]
    ff_local = hidden.shape[2]
    groups = lax.axis_size("expert")
    experts = groups * EXP_DEV
    most_rows = 3 * tok_rows // 4
    labels = jnp.arange(experts, dtype=jnp.int32)
    routed = routes[:, :, None] == labels[None, None, :]
    local_load = jnp.sum(jnp.where(routed & within[:, None, None], 1.0, 0.0), axis=(0, 1)).astype(
        jnp.float32
    )
    flat_rows = tok_rows * route_top
    flat_hits = routed.reshape(flat_rows, experts).astype(jnp.int32)
    rank_of = jnp.sum((jnp.cumsum(flat_hits, axis=0) - 1) * flat_hits, axis=1)
    slot_of = routes.reshape(flat_rows) * most_rows + rank_of
    source = (
        jnp.zeros((experts * most_rows,), jnp.int32)
        .at[slot_of]
        .set(jnp.arange(flat_rows, dtype=jnp.int32))
    )
    filled = jnp.zeros((experts * most_rows,), jnp.float32).at[slot_of].set(1.0)
    token_of = source // route_top
    slot_weight = jnp.take(weight.reshape(flat_rows), source) * filled
    packed_h = jnp.take(hidden.reshape(flat_rows, ff_local), source, axis=0).reshape(
        groups, EXP_DEV * most_rows, ff_local
    )
    narrow_s = (
        slot_weight[:, None] * jnp.take(cotangent, token_of, axis=0).astype(jnp.float32)
    ).astype(jnp.bfloat16)
    moved_h, narrow = (
        lax.all_to_all(packed_h, "expert", split_axis=0, concat_axis=0, tiled=True),
        lax.all_to_all(
            narrow_s.reshape(groups, EXP_DEV * most_rows, cotangent.shape[1]),
            "expert",
            split_axis=0,
            concat_axis=0,
            tiled=True,
        ),
    )
    moved_s = lax.all_gather(narrow, "mp", axis=2, tiled=True)
    moved_h = moved_h.reshape(groups, EXP_DEV, most_rows, ff_local)
    moved_s = moved_s.reshape(groups, EXP_DEV, most_rows, moved_s.shape[2])
    products = [
        lax.dot_general(
            moved_h[:, 0],
            moved_s[:, 0],
            (((0, 1), (0, 1)), ((), ())),
            preferred_element_type=jnp.float32,
        )
    ]
    owned = lax.psum_scatter(jnp.stack(products, axis=1), "dp", scatter_dimension=0, tiled=True)
    grad_down = jnp.transpose(owned, (1, 0, 2))
    expert_load = lax.psum(local_load, ("dp", "expert"))
    return (grad_down, expert_load)


def solution(mesh):
    in_specs = (
        P(("dp", "expert"), None, "mp"),
        P(("dp", "expert"), "mp"),
        P(("dp", "expert"), None),
        P(("dp", "expert"), None),
        P(("dp", "expert"), None),
        P(("dp", "expert"), None),
        P(("dp", "expert"), None),
    )
    out_specs = (P("expert", ("mp", "dp"), None), P())
    return jax.shard_map(body, mesh=mesh, in_specs=in_specs, out_specs=out_specs, check_vma=False)
```

profile of v0, /device:TPU:0, one launch (start us, length us, event | category | flops | bytes accessed | tf_op | source)
XLA Modules:
  0.0 187.8 jit_solution(6503914561430639834)
XLA Ops:
  7.2 0.0 copy-start
  7.2 0.0 all-gather.2.cloned.1.call-start
  7.2 0.8 fusion.6
  8.0 0.1 slice.15
  8.1 0.1 slice.14
  8.2 0.7 fusion.14
  8.9 0.7 broadcast_multiply_fusion.1
  9.6 0.8 copy.16
  10.4 0.1 eq.83
  10.6 0.1 eq.79
  10.7 0.1 copy.15
  10.9 0.2 mul.49
  11.0 1.1 reduce-window.6
  12.2 0.2 slice_reduce_fusion
  12.4 0.2 reduce-window.9
  12.6 0.1 add_bitcast_fusion
  12.7 3.4 %scatter_custom_fusion = s32[1152]{0:T(1024)S(1)} fusion(s32[768]{0:T(1024)S(1)} %fusion.11, s32[768]{0:T(1024)S(1)} %iota.36, s32[]{:T(128)} %constant.86.clone.1), kind=kCustom, calls=%fused_computation.39 | custom fusion | bytes 4612 | tf_op jit(solution)/shard_map/scatter | solution.py:51
  16.2 0.1 fusion.12
  16.3 0.7 fusion.13
  16.9 0.1 broadcast_reduce_fusion
  17.0 0.1 broadcast_in_dim.116
  17.1 0.7 broadcast_reduce_fusion.1
  17.8 0.1 lt.66
  17.9 0.1 lt.64
  18.0 0.7 broadcast_multiply_fusion
  18.7 0.1 copy.18
  18.9 0.1 reshape.294
  19.0 3.4 %scatter_custom_fusion.1 = f32[1152]{0:T(1024)S(1)} fusion(s32[768]{0:T(1024)S(1)} %fusion.11, f32[768]{0:T(1024)S(1)} %broadcast.245, f32[]{:T(128)} %constant.96.clone.1), kind=kCustom, calls=%fused_computation.37 | custom fusion | bytes 4612 | tf_op jit(solution)/shard_map/scatter | solution.py:53
  22.4 4.6 %gather_fusion.1 = f32[1152]{0:T(1024)S(1)} fusion(f32[768]{0:T(1024)S(1)} %reshape.294, s32[2048]{0:T(1024)S(1)} %pad_clamp_fusion.1), kind=kCustom, calls=%fused_computation.1 | custom fusion | bytes 13824 | tf_op jit(solution)/shard_map/jit(_take)/gather | solution.py:55
  27.0 0.1 mul.56
  27.1 0.1 broadcast_in_dim.121
  27.2 4.2 %gather_fusion.2 = bf16[1152,512]{1,0:T(8,128)(2,1)S(1)} fusion(bf16[384,512]{1,0:T(8,128)(2,1)S(1)} %copy-done, s32[2048]{0:T(1024)S(1)} %pad_clamp_fusion), kind=kCustom, calls=%fused_computation.2 | custom fusion | bytes 2363904 | tf_op jit(solution)/shard_map/jit(_take)/gather | solution.py:60
  31.5 0.4 multiply_convert_fusion
  31.8 20.6 %all_to_all.10 = bf16[4,288,512]{2,1,0:T(8,128)(2,1)} all-to-all(bf16[4,288,512]{2,1,0:T(8,128)(2,1)S(1)} %multiply_convert_fusion), channel_id=1, replica_groups=mesh['dp'=2,'expert'=4,'mp'=4] {'expert'}, dimensions={0} | all-to-all | bytes 2359296 | tf_op jit(solution)/shard_map/all_to_all | solution.py:64
  52.5 0.0 all-gather.2.cloned.1.call-update
  52.5 0.0 reduce-scatter.2.cloned.1.call-start
  52.5 0.1 broadcast_in_dim.106
  52.6 5.7 %reshape.293 = bf16[768,1792]{1,0:T(8,128)(2,1)S(1)} reshape(bf16[384,2,1792]{2,1,0:T(2,128)(2,1)} %param.7) | data formatting | bytes 5505024 | tf_op jit(solution)/shard_map/reshape | solution.py:56
  58.4 5.6 %gather_fusion = bf16[1152,1792]{1,0:T(8,128)(2,1)} fusion(bf16[768,1792]{1,0:T(8,128)(2,1)S(1)} %reshape.293, s32[2048]{0:T(1024)S(1)} %pad_clamp_fusion.1), kind=kCustom, calls=%fused_computation | custom fusion | bytes 8262144 | tf_op jit(solution)/shard_map/jit(_take)/gather | solution.py:56
  64.0 2.6 %broadcast_select_fusion = bf16[4,288,1792]{2,1,0:T(8,128)(2,1)S(1)} fusion(bf16[4,288,1792]{2,1,0:T(8,128)(2,1)} %bitcast.39, pred[4,288]{1,0:T(4,128)(4,1)S(1)} %broadcast_in_dim.106), kind=kLoop, calls=%fused_computation.6 | loop fusion | flops 2064384 | bytes 8258688 | tf_op jit(solution)/shard_map/jit(_take)/select_n | solution.py:56
  66.6 49.7 %all_to_all.11 = bf16[4,288,1792]{2,1,0:T(8,128)(2,1)} all-to-all(bf16[4,288,1792]{2,1,0:T(8,128)(2,1)S(1)} %broadcast_select_fusion), channel_id=1, replica_groups=mesh['dp'=2,'expert'=4,'mp'=4] {'expert'}, dimensions={0} | all-to-all | bytes 8257536 | tf_op jit(solution)/shard_map/all_to_all | solution.py:63
  116.4 25.4 %all-gather.2.cloned.1.call-done = bf16[4,288,2048]{2,1,0:T(8,128)(2,1)} async-done(((bf16[4,288,512]{2,1,0:T(8,128)(2,1)}), bf16[4,288,2048]{2,1,0:T(8,128)(2,1)}) %all-gather.2.cloned.1.call-update) | async-done | bytes 4718608 | tf_op jit(solution)/shard_map/all_gather | solution.py:72
  141.8 15.8 %convolution_bitcast_fusion = f32[1792,1,2048]{2,0,1:T(8,128)} fusion(bf16[4,288,1792]{2,1,0:T(8,128)(2,1)} %all_to_all.11, bf16[4,288,2048]{2,1,0:T(8,128)(2,1)} %all-gather.2.cloned.1.call-done), kind=kOutput, calls=%fused_computation.5 | convolution fusion | flops 8455716864 | bytes 23527424 | tf_op jit(solution)/shard_map/dot_general | solution.py:76
  157.5 0.0 reduce-scatter.2.cloned.1.call-update
  157.6 0.7 copy-done.1
  158.2 0.1 select_reduce_fusion
  158.3 14.8 %psum.7 = f32[4]{0:T(128)} all-reduce(f32[4]{0:T(128)S(1)} %select_reduce_fusion), channel_id=1, replica_groups=mesh['dp'=2,'expert'=4,'mp'=4] {'dp','expert'}, use_global_device_ids=true, to_apply=%region_9.10 | all-reduce | flops 4 | bytes 32 | tf_op jit(solution)/shard_map/psum | solution.py:85
  173.1 7.8 %reduce-scatter.2.cloned.1.call-done = f32[896,1,2048]{2,0,1:T(8,128)} async-done(((f32[1792,1,2048]{2,0,1:T(8,128)}), f32[896,1,2048]{2,0,1:T(8,128)}) %reduce-scatter.2.cloned.1.call-update) | async-done | bytes 7340048 | tf_op jit(solution)/shard_map/reduce_scatter | solution.py:83
  (15 shorter events, 0.1 us)
Async XLA Ops:
  7.2 20.0 %copy-start = (bf16[384,512]{1,0:T(8,128)(2,1)S(1)}, bf16[384,512]{1,0:T(8,128)(2,1)}, u32[]{:S(2)}) copy-start(bf16[384,512]{1,0:T(8,128)(2,1)} %param.8) | copy-start | bytes 1179652
  7.2 134.6 %all-gather.2.cloned.1.call-start = ((), (), s32[]{:S(2)}) async-start(), calls=%async_computation.3 | async-start | bytes 5898240 | tf_op jit(solution)/shard_map/all_gather | solution.py:72
  52.5 128.4 %reduce-scatter.2.cloned.1.call-start = ((), (), s32[]{:S(2)}) async-start(), calls=%async_computation.4 | async-start | bytes 22020096 | tf_op jit(solution)/shard_map/reduce_scatter | solution.py:83
  157.5 0.7 copy-start.1
Sparse Core Ops, SparseCore 0:
  52.6 89.0 all-gather.1
  157.7 23.2 reduce-scatter.1
where the time goes:
time: 188 us
  blocking collectives  85.2 us (45%)
  waiting for transfers between devices  33.3 us (18%)
  local copies, waits for them, and re-layouts  31 us (16%)
  matrix products  15.8 us (8%)
  between operations  14.3 us (8%)
  other arithmetic  8.25 us (4%)
    all_to_all x1, blocking collectives, body(): lax.all_to_all(packed_h, 'expert', split_axis=0, concat_axis=0, tiled=True)  49.7 us
    all_gather x1, waiting for transfers between devices, body(): moved_s = lax.all_gather(narrow, 'mp', axis=2, tiled=True)  25.4 us
    all_to_all x1, blocking collectives, body(): lax.all_to_all(narrow_s.reshape(groups, EXP_DEV * most_rows, cotangent.sh...  20.6 us
    dot_general x1, matrix products, body(): lax.dot_general(moved_h[:, 0], moved_s[:, 0], (((0, 1), (0, 1)), ((), ())...  15.8 us
    psum x1, blocking collectives, body(): expert_load = lax.psum(local_load, ('dp', 'expert'))  14.8 us
    reduce_scatter x1, waiting for transfers between devices, body(): lax.psum_scatter(jnp.stack(products, axis=1), 'dp', scatter_dimension=0,...  7.84 us
    reshape x1, local copies, waits for them, and re-layouts, body(): hidden.reshape(flat_rows, ff_local)  5.71 us
    gather x1, local copies, waits for them, and re-layouts, body(): jnp.take(hidden.reshape(flat_rows, ff_local), source, axis=0)  5.63 us
  transfers between devices with their start and end apart: 2, of which 2 were waited for; matrix products, arithmetic and copies ran while one was open for 8% of the time, Pallas kernels for 0%

commit v1 on v0

--- a/solution.py
+++ b/solution.py
@@ -1,16 +1,23 @@
+import functools
+
 import jax
 import jax.numpy as jnp
 from jax import lax
+from jax.experimental import pallas as pl
+from jax.experimental.pallas import tpu as pltpu
 from jax.sharding import PartitionSpec as P
 
 EXP_DEV = 1
 LEN = 32
+LANES = 128
+VMEM_ROOM = 48 * 1024 * 1024
+MESH = pl.DeviceIdType.MESH
 
 
 beta_scale = 0.1
 
 
-def token_weights(combine, block_pair, lengths, log_ratio, block_len):
+def token_factors(block_pair, lengths, log_ratio, block_len):
     blocks = block_pair.shape[1]
     labels = jnp.arange(blocks, dtype=jnp.int32)
     matches = block_pair[:, :, None] == labels[None, None, :]
@@ -25,11 +32,311 @@
     position = jnp.arange(block_len, dtype=jnp.int32)
     within = position[None, None, :] < lengths[:, :, None]
     per_token = jnp.where(within, block_weight[:, :, None], 0.0).reshape(-1)
-    return (combine * per_token[:, None], within.reshape(-1))
-
-
-def body(hidden, cotangent, routes, combine, block_pair, lengths, log_ratio):
-    weight, within = token_weights(combine, block_pair, lengths, log_ratio, LEN)
+    return per_token, within.reshape(-1)
+
+
+def exchange_kernel(
+    dims, h_ref, cot_ref, routes_ref, flat_ref, weight_ref, live_ref,
+    hr, sa, sb, load_ref,
+    hs, sas, sbs, cotb, lbuf,
+    xa_s, a_r, up_s, dn_s, dd_s, cb_s, cb_r, xb_s, b_r, db_s, h_s, h_r, l_s, l_r,
+):
+    nd, ne, nm, most, ca, cb = dims
+    d, e, m = lax.axis_index("dp"), lax.axis_index("expert"), lax.axis_index("mp")
+    toks, ff = h_ref.shape[0] // 2, h_ref.shape[1]
+    half = ff // nd
+    me = d * ne + e
+
+    def dev(dd=None, ee=None, mm=None):
+        return {"dp": d if dd is None else dd, "expert": e if ee is None else ee, "mp": m if mm is None else mm}
+
+    def remote(src, dst, ssem, rsem, where):
+        return pltpu.make_async_remote_copy(
+            src_ref=src, dst_ref=dst, send_sem=ssem, recv_sem=rsem, device_id=where, device_id_type=MESH
+        )
+
+    barrier = pltpu.get_barrier_semaphore()
+    peers = [
+        dev(dd=lax.rem(d + i, nd), ee=lax.rem(e + j, ne)) for i in range(nd) for j in range(ne) if i or j
+    ] + [dev(mm=lax.rem(m + i, nm)) for i in range(1, nm)]
+    for peer in peers:
+        pl.semaphore_signal(barrier, inc=1, device_id=peer, device_id_type=MESH)
+
+    def ranks(named, n):
+        before = lax.broadcasted_iota(jnp.int32, (n, n), 0) < lax.broadcasted_iota(jnp.int32, (n, n), 1)
+        rank = jnp.dot(
+            jnp.where(named, 1.0, 0.0).astype(jnp.bfloat16),
+            jnp.where(before, 1.0, 0.0).astype(jnp.bfloat16),
+            preferred_element_type=jnp.float32,
+        )
+        return jnp.where(named, rank, -1.0).astype(jnp.int32)
+
+    rows8 = -(-ne // 8) * 8
+    row_id = lax.broadcasted_iota(jnp.int32, (rows8, 1), 0)
+    owner = jnp.where(row_id < ne, lax.rem(row_id + e, ne), -1)
+    hit0 = routes_ref[0:1, :] == owner
+    hit1 = routes_ref[1:2, :] == owner
+    named = hit0 | hit1
+    tok_pos = ranks(named, toks)
+    tok_weight = jnp.where(hit0, weight_ref[0:1, :], 0.0) + jnp.where(hit1, weight_ref[1:2, :], 0.0)
+    in_order = (routes_ref[0:1, :] == row_id) | (routes_ref[1:2, :] == row_id)
+    counts = jnp.sum(jnp.where(in_order, live_ref[...], 0.0), axis=1, keepdims=True)
+    lbuf[me] = jnp.broadcast_to(counts, (rows8, LANES))
+
+    slot_tok = lax.broadcasted_iota(jnp.int32, (most, toks), 0)
+    picks, scales = [], []
+    for j in range(ne):
+        hit = slot_tok == tok_pos[j : j + 1, :]
+        picks.append(jnp.where(hit, 1.0, 0.0).astype(jnp.bfloat16))
+        scales.append(jnp.sum(jnp.where(hit, tok_weight[j : j + 1, :], 0.0), axis=1, keepdims=True))
+
+    def pack_s(j, rows):
+        rows = jnp.dot(picks[j], rows, preferred_element_type=jnp.float32)
+        return (scales[j] * rows).astype(jnp.bfloat16)
+
+    sends = []
+    for j in range(ne):
+        block = pack_s(j, cot_ref[:, :ca])
+        if j == 0:
+            sa[m, me] = block
+        else:
+            sas[j] = block
+    cotb[m] = cot_ref[:, ca:]
+
+    pl.semaphore_wait(barrier, len(peers))
+
+    for j in range(1, ne):
+        copy = remote(sas.at[j], sa.at[m, me], xa_s.at[j], a_r.at[m, me], dev(ee=lax.rem(e + j, ne)))
+        copy.start()
+        sends.append(copy)
+    for i in range(1, nm):
+        copy = remote(cot_ref.at[:, pl.ds(ca, cb)], cotb.at[m], cb_s.at[i], cb_r.at[m], dev(mm=lax.rem(m + i, nm)))
+        copy.start()
+        sends.append(copy)
+    n = 0
+    for i in range(nd):
+        for j in range(ne):
+            if i or j:
+                copy = remote(
+                    lbuf.at[me], lbuf.at[me], l_s.at[n], l_r.at[me], dev(dd=lax.rem(d + i, nd), ee=lax.rem(e + j, ne))
+                )
+                copy.start()
+                sends.append(copy)
+                n += 1
+
+    guarded = []
+
+    def forward(q, src, up, down, ek):
+        block = sa.at[q, src]
+        cu = remote(block, block, up_s.at[q, ek], a_r.at[q, src], dev(mm=lax.rem(m + 1, nm)))
+        cd = remote(block, block, dn_s.at[q, ek], a_r.at[q, src], dev(mm=lax.rem(m + nm - 1, nm)))
+
+        @pl.when(up)
+        def _():
+            cu.start()
+
+        @pl.when(down)
+        def _():
+            cd.start()
+
+        guarded.append((up, cu))
+        guarded.append((down, cd))
+
+    def to_partners(q, src, ek, guard=None):
+        for i in range(1, nd):
+            c = remote(sa.at[q, src], sa.at[q, src], dd_s.at[q, i - 1, ek], a_r.at[q, src], dev(dd=lax.rem(d + i, nd)))
+            if guard is None:
+                c.start()
+                sends.append(c)
+            else:
+                pl.when(guard)(c.start)
+                guarded.append((guard, c))
+
+    forward(m, me, m + 1 < nm, m > 0, e)
+    to_partners(m, me, e)
+
+    slot_flat = lax.broadcasted_iota(jnp.int32, (most, 2 * toks), 0)
+    flat_pos = ranks(flat_ref[...] == owner, 2 * toks)
+    for j in [*range(1, ne), 0]:
+        pick = jnp.where(slot_flat == flat_pos[j : j + 1, :], 1.0, 0.0).astype(jnp.bfloat16)
+        for c in range(nd):
+            cols = pl.ds(c * half, half)
+            hs[j, c] = jnp.dot(pick, h_ref[:, cols], preferred_element_type=jnp.float32).astype(jnp.bfloat16)
+        for i in range(nd):
+            to = lax.rem(d + i, nd)
+            if i or j:
+                copy = remote(
+                    hs.at[j, to], hr.at[me], h_s.at[j, i], h_r.at[me], dev(dd=to, ee=lax.rem(e + j, ne))
+                )
+                copy.start()
+                sends.append(copy)
+    hr[me] = hs[0, d]
+
+    def wait_in(buf, sem, guard=None):
+        c = pltpu.make_async_copy(buf, buf, sem)
+        if guard is None:
+            c.wait()
+        else:
+            pl.when(guard)(c.wait)
+
+    for i in range(1, nm):
+        q = lax.rem(m + i, nm)
+        wait_in(cotb.at[q], cb_r.at[q])
+    dense = jnp.concatenate([cotb[q] for q in range(nm)], axis=1)
+    for j in range(ne):
+        block = pack_s(j, dense)
+        if j == 0:
+            sb[me] = block
+            for i in range(1, nd):
+                copy = remote(sb.at[me], sb.at[me], db_s.at[i - 1, 0], b_r.at[me], dev(dd=lax.rem(d + i, nd)))
+                copy.start()
+                sends.append(copy)
+        else:
+            sbs[j] = block
+            copy = remote(sbs.at[j], sb.at[me], xb_s.at[j], b_r.at[me], dev(ee=lax.rem(e + j, ne)))
+            copy.start()
+            sends.append(copy)
+
+    for j in range(1, ne):
+        ej = lax.rem(e + j, ne)
+        src = d * ne + ej
+        wait_in(sa.at[m, src], a_r.at[m, src])
+        forward(m, src, m + 1 < nm, m > 0, ej)
+        to_partners(m, src, ej)
+    for k in range(1, nm):
+        below, above = m - k, m + k
+        ql, qh = lax.rem(below + nm, nm), lax.rem(above, nm)
+        never = m < 0
+        for j in range(ne):
+            ej = lax.rem(e + j, ne)
+            src = d * ne + ej
+            wait_in(sa.at[ql, src], a_r.at[ql, src], below >= 0)
+            c = remote(sa.at[ql, src], sa.at[ql, src], up_s.at[ql, ej], a_r.at[ql, src], dev(mm=lax.rem(m + 1, nm)))
+            go = (below >= 0) & (m + 1 < nm)
+            pl.when(go)(c.start)
+            guarded.append((go, c))
+            to_partners(ql, src, ej, below >= 0)
+            wait_in(sa.at[qh, src], a_r.at[qh, src], above < nm)
+            c = remote(sa.at[qh, src], sa.at[qh, src], dn_s.at[qh, ej], a_r.at[qh, src], dev(mm=lax.rem(m + nm - 1, nm)))
+            go = (above < nm) & (m > 0)
+            pl.when(go)(c.start)
+            guarded.append((go, c))
+            to_partners(qh, src, ej, above < nm)
+
+    for j in range(1, ne):
+        src = d * ne + lax.rem(e + j, ne)
+        wait_in(sb.at[src], b_r.at[src])
+        for i in range(1, nd):
+            copy = remote(sb.at[src], sb.at[src], db_s.at[i - 1, j], b_r.at[src], dev(dd=lax.rem(d + i, nd)))
+            copy.start()
+            sends.append(copy)
+
+    for i in range(1, nd):
+        other = lax.rem(d + i, nd)
+        for j in range(ne):
+            src = other * ne + j
+            wait_in(sb.at[src], b_r.at[src])
+            for q in range(nm):
+                wait_in(sa.at[q, src], a_r.at[q, src])
+    for i in range(nd):
+        for j in range(ne):
+            if i or j:
+                src = lax.rem(d + i, nd) * ne + lax.rem(e + j, ne)
+                wait_in(hr.at[src], h_r.at[src])
+                wait_in(lbuf.at[src], l_r.at[src])
+    total = lbuf[0]
+    for k in range(1, nd * ne):
+        total = total + lbuf[k]
+    load_ref[...] = total
+
+    for c in sends:
+        c.wait_send()
+    for go, c in guarded:
+        pl.when(go)(c.wait_send)
+
+
+def product_kernel(h_ref, sa_ref, sb_ref, out_ref, turned):
+    @pl.when(pl.program_id(0) == 0)
+    def _():
+        turned[...] = h_ref[...].T
+
+    rows = jnp.concatenate([sa_ref[0], sb_ref[...]], axis=1)
+    out_ref[0] = jnp.dot(turned[...], rows, preferred_element_type=jnp.float32)
+
+
+def fast_body(hidden, cotangent, routes, combine, block_pair, lengths, log_ratio):
+    nd, ne, nm = lax.axis_size("dp"), lax.axis_size("expert"), lax.axis_size("mp")
+    per_token, within = token_factors(block_pair, lengths, log_ratio, LEN)
+    toks, top, ff = hidden.shape
+    width = cotangent.shape[1]
+    most = 3 * toks // 4
+    cb = width // 4 // LANES * LANES
+    ca = width - cb
+    half = ff // nd
+    srcs = nd * ne
+    rows8 = -(-ne // 8) * 8
+    dims = (nd, ne, nm, most, ca, cb)
+    bf16, f32 = jnp.bfloat16, jnp.float32
+    routes_t = routes.T
+    weight_t = combine.T * per_token[None, :]
+    live = jnp.where(within, 1.0, 0.0).astype(f32)[None, :]
+    vmem = pl.BlockSpec(memory_space=pltpu.VMEM)
+    dma = pltpu.SemaphoreType.DMA
+    hr, sa, sb, load = pl.pallas_call(
+        functools.partial(exchange_kernel, dims),
+        out_shape=(
+            jax.ShapeDtypeStruct((srcs, most, half), bf16),
+            jax.ShapeDtypeStruct((nm, srcs, most, ca), bf16),
+            jax.ShapeDtypeStruct((srcs, most, nm * cb), bf16),
+            jax.ShapeDtypeStruct((rows8, LANES), f32),
+        ),
+        in_specs=[vmem] * 6,
+        out_specs=(vmem,) * 4,
+        scratch_shapes=[
+            pltpu.VMEM((ne, nd, most, half), bf16),
+            pltpu.VMEM((ne, most, ca), bf16),
+            pltpu.VMEM((ne, most, nm * cb), bf16),
+            pltpu.VMEM((nm, toks, cb), bf16),
+            pltpu.VMEM((srcs, rows8, LANES), f32),
+            dma((ne,)),
+            dma((nm, srcs)),
+            dma((nm, ne)),
+            dma((nm, ne)),
+            dma((nm, nd, ne)),
+            dma((nm,)),
+            dma((nm,)),
+            dma((ne,)),
+            dma((srcs,)),
+            dma((nd, ne)),
+            dma((ne, nd)),
+            dma((srcs,)),
+            dma((srcs,)),
+            dma((srcs,)),
+        ],
+        compiler_params=pltpu.CompilerParams(
+            collective_id=0, has_side_effects=True, vmem_limit_bytes=VMEM_ROOM
+        ),
+    )(hidden.reshape(toks * top, ff), cotangent, routes_t, routes.reshape(1, toks * top), weight_t, live)
+    depth = srcs * most
+    grad_down = pl.pallas_call(
+        product_kernel,
+        out_shape=jax.ShapeDtypeStruct((1, half, nm * width), f32),
+        grid=(nm,),
+        in_specs=[
+            pl.BlockSpec((depth, half), lambda q: (0, 0)),
+            pl.BlockSpec((1, depth, ca), lambda q: (q, 0, 0)),
+            pl.BlockSpec((depth, cb), lambda q: (0, q)),
+        ],
+        out_specs=pl.BlockSpec((1, half, width), lambda q: (0, 0, q)),
+        scratch_shapes=[pltpu.VMEM((half, depth), bf16)],
+        compiler_params=pltpu.CompilerParams(vmem_limit_bytes=VMEM_ROOM),
+    )(hr.reshape(depth, half), sa.reshape(nm, depth, ca), sb.reshape(depth, nm * cb))
+    return grad_down, load[:ne, 0]
+
+
+def plain_body(hidden, cotangent, routes, combine, block_pair, lengths, log_ratio):
+    per_token, within = token_factors(block_pair, lengths, log_ratio, LEN)
+    weight = combine * per_token[:, None]
     tok_rows = routes.shape[0]
     route_top = routes.shape[1]
     ff_local = hidden.shape[2]
@@ -97,4 +404,11 @@
         P(("dp", "expert"), None),
     )
     out_specs = (P("expert", ("mp", "dp"), None), P())
+
+    def body(hidden, cotangent, *rest):
+        rows = mesh.shape["dp"] * mesh.shape["expert"] * (3 * hidden.shape[0] // 4)
+        bytes_in = 2 * rows * (cotangent.shape[1] * mesh.shape["mp"] + hidden.shape[2])
+        run = fast_body if 2 * bytes_in < VMEM_ROOM else plain_body
+        return run(hidden, cotangent, *rest)
+
     return jax.shard_map(body, mesh=mesh, in_specs=in_specs, out_specs=out_specs, check_vma=False)

time: 188 us -> 109 us (0.58)
  Pallas kernels: 0 us -> 96.1 us
  blocking collectives: 85.2 us -> 0 us
  waiting for transfers between devices: 33.3 us -> 0 us
  local copies, waits for them, and re-layouts: 31 us -> 8.73 us
  matrix products: 15.8 us -> 0 us
  between operations: 14.3 us -> 0.71 us
  other arithmetic: 8.25 us -> 2.98 us
    pallas_call x0 -> x2, Pallas kernels: none -> 96.1 us  [the longest x1 81.6 us: fast_body(): pl.pallas_call(functools.partial(exchange_kernel, dims), out_shape=(jax.S...]
    all_to_all x2 -> x0, blocking collectives: 70.4 us -> none  [the longest x1 49.7 us: body(): lax.all_to_all(packed_h, 'expert', split_axis=0, concat_axis=0, tiled=True)]
    all_gather x1 -> x0, waiting for transfers between devices: 25.4 us -> none  [body(): moved_s = lax.all_gather(narrow, 'mp', axis=2, tiled=True)]
    dot_general x1 -> x0, matrix products: 15.8 us -> none  [body(): lax.dot_general(moved_h[:, 0], moved_s[:, 0], (((0, 1), (0, 1)), ((), ())...]
    psum x1 -> x0, blocking collectives: 14.8 us -> none  [body(): expert_load = lax.psum(local_load, ('dp', 'expert'))]
    gather x3 -> x0, local copies, waits for them, and re-layouts: 14.4 us -> none  [the longest x1 5.63 us: body(): jnp.take(hidden.reshape(flat_rows, ff_local), source, axis=0)]
    reduce_scatter x1 -> x0, waiting for transfers between devices: 7.84 us -> none  [body(): lax.psum_scatter(jnp.stack(products, axis=1), 'dp', scatter_dimension=0,...]
    scatter x2 -> x0, local copies, waits for them, and re-layouts: 6.77 us -> none  [the longest x1 3.38 us: body(): filled = jnp.zeros((experts * most_rows,), jnp.float32).at[slot_of].set(1.0)]
  transfers between devices with their start and end apart: 2 -> 0, of which waited for: 2 -> 0; matrix products, arithmetic and copies ran while one was open for 8% -> 0% of each run, Pallas kernels for 0% -> 0%
where the time goes in v1:
time: 109 us
  Pallas kernels  96.1 us (88%)
  local copies, waits for them, and re-layouts  8.73 us (8%)
  other arithmetic  2.98 us (3%)
    pallas_call x1, Pallas kernels, fast_body(): pl.pallas_call(functools.partial(exchange_kernel, dims), out_shape=(jax.S...  81.6 us
    pallas_call x1, Pallas kernels, fast_body(): pl.pallas_call(product_kernel, out_shape=jax.ShapeDtypeStruct((1, half, n...  14.5 us
    reshape x1, local copies, waits for them, and re-layouts, fast_body(): hidden.reshape(toks * top, ff)  5.71 us

profile of v1, /device:TPU:0, one launch (start us, length us, event | category | flops | bytes accessed | tf_op | source)
XLA Modules:
  0.0 108.5 jit_solution(11370823943089561828)
XLA Ops:
  0.6 0.0 copy-start.1
  0.6 0.0 copy-start
  0.7 0.8 fusion
  1.5 0.1 slice.10
  1.6 0.1 slice.9
  1.7 0.7 fusion.3
  2.4 0.1 fusion.1
  2.5 0.7 fusion.2
  3.1 0.1 broadcast_reduce_fusion
  3.2 0.1 broadcast_in_dim.64
  3.3 0.7 lt.47
  4.0 0.1 lt.53
  4.1 0.1 lt.48
  4.2 0.1 lt.52
  4.3 0.1 lt.46
  4.4 0.7 multiply_bitcast_fusion.weight_ref
  5.1 0.8 copy.11
  5.9 0.2 reshape.236.flat_ref
  6.0 5.7 %reshape.235.h_ref = bf16[768,1792]{1,0:T(8,128)(2,1)S(1)} reshape(bf16[384,2,1792]{2,1,0:T(2,128)(2,1)} %param.7) | data formatting | bytes 5505024 | tf_op jit(solution)/shard_map/reshape | solution.py:319
  11.8 0.0 copy-done.1
  11.8 0.0 copy-done
  11.8 81.6 %shard_map.95 = (bf16[8,288,896]{2,1,0:T(8,128)(2,1)}, bf16[4,8,288,384]{3,2,1,0:T(8,128)(2,1)}, bf16[8,288,512]{2,1,0:T(8,128)(2,1)S(1)}, f32[8,128]{1,0:T(8,128)S(1)}) custom-call(bf16[768,1792]{1,0:T(8,128)(2,1)S(1)} %reshape.235.h_ref, bf16[384,512]{1,0:T(8,128)(2,1)S(1)} %copy-done, s32[2,384]{1,0:T(2,128)S(1)} %bitcast.25, ...), custom_call_target="tpu_custom_call" | custom-call | tf_op jit(solution)/shard_map/pallas_call | solution.py:285
  93.4 14.5 %shard_map.96 = f32[1,896,2048]{2,1,0:T(8,128)} custom-call(bf16[2304,896]{1,0:T(8,128)(2,1)} %bitcast.27, bf16[4,2304,384]{2,1,0:T(8,128)(2,1)} %bitcast.26, bf16[2304,512]{1,0:T(8,128)(2,1)S(1)} %bitcast.24), custom_call_target="tpu_custom_call" | custom-call | tf_op jit(solution)/shard_map/pallas_call | solution.py:321
  107.9 0.6 slice_reduce_fusion
  (5 shorter events, 0.0 us)
Async XLA Ops:
  0.6 11.1 %copy-start.1 = (s32[384,2]{0,1:T(2,128)S(1)}, s32[384,2]{0,1:T(2,128)}, u32[]{:S(2)}) copy-start(s32[384,2]{0,1:T(2,128)} %param.9) | copy-start | bytes 9220
  0.6 11.1 %copy-start = (bf16[384,512]{1,0:T(8,128)(2,1)S(1)}, bf16[384,512]{1,0:T(8,128)(2,1)}, u32[]{:S(2)}) copy-start(bf16[384,512]{1,0:T(8,128)(2,1)} %cot_ref.1) | copy-start | bytes 1179652

commit v2 on v1

--- a/solution.py
+++ b/solution.py
@@ -36,14 +36,15 @@
 
 
 def exchange_kernel(
-    dims, h_ref, cot_ref, routes_ref, flat_ref, weight_ref, live_ref,
+    dims, h_hbm, cot_hbm, routes_hbm, combine_hbm, pair_hbm, len_hbm, ratio_hbm,
     hr, sa, sb, load_ref,
-    hs, sas, sbs, cotb, lbuf,
+    h_in, cot_ref, routes_ref, combine_ref, pair_ref, len_ref, ratio_ref,
+    hs, sas, sbs, cotb, lbuf, in_sem,
     xa_s, a_r, up_s, dn_s, dd_s, cb_s, cb_r, xb_s, b_r, db_s, h_s, h_r, l_s, l_r,
 ):
     nd, ne, nm, most, ca, cb = dims
     d, e, m = lax.axis_index("dp"), lax.axis_index("expert"), lax.axis_index("mp")
-    toks, ff = h_ref.shape[0] // 2, h_ref.shape[1]
+    toks, top, ff = h_in.shape
     half = ff // nd
     me = d * ne + e
 
@@ -55,6 +56,15 @@
             src_ref=src, dst_ref=dst, send_sem=ssem, recv_sem=rsem, device_id=where, device_id_type=MESH
         )
 
+    loads = [
+        pltpu.make_async_copy(src, dst, in_sem.at[i])
+        for i, (src, dst) in enumerate((
+            (pair_hbm, pair_ref), (len_hbm, len_ref), (ratio_hbm, ratio_ref), (routes_hbm, routes_ref),
+            (combine_hbm, combine_ref), (cot_hbm, cot_ref), (h_hbm, h_in),
+        ))
+    ]
+    for load in loads:
+        load.start()
     barrier = pltpu.get_barrier_semaphore()
     peers = [
         dev(dd=lax.rem(d + i, nd), ee=lax.rem(e + j, ne)) for i in range(nd) for j in range(ne) if i or j
@@ -69,7 +79,34 @@
             jnp.where(before, 1.0, 0.0).astype(jnp.bfloat16),
             preferred_element_type=jnp.float32,
         )
-        return jnp.where(named, rank, -1.0).astype(jnp.int32)
+        return jnp.where(named, rank, -1.0)
+
+    for load in loads[:-1]:
+        load.wait()
+
+    blocks = pair_ref.shape[1]
+    block_len = toks // blocks
+    square = (blocks, blocks)
+    diagonal = lax.broadcasted_iota(jnp.int32, square, 0) == lax.broadcasted_iota(jnp.int32, square, 1)
+
+    def column(row):
+        return jnp.sum(jnp.where(diagonal, row, 0.0), axis=1, keepdims=True)
+
+    pair, ratio = pair_ref[...], ratio_ref[...]
+    chosen = lax.rem(pair, 2) == 0
+    other_side = jnp.where(chosen, pair + 1, pair - 1)
+    is_other = column(pair.astype(jnp.float32)) == other_side.astype(jnp.float32)
+    other_ratio = jnp.sum(jnp.where(is_other, column(ratio), 0.0), axis=0, keepdims=True)
+    margin = jnp.where(chosen, ratio - other_ratio, other_ratio - ratio)
+    coef = beta_scale * (1.0 / (1.0 + jnp.exp(beta_scale * margin)))
+    block_weight = column(jnp.where(chosen, -coef, coef))
+    token_id = lax.broadcasted_iota(jnp.int32, (blocks, toks), 1)
+    place = token_id - block_len * lax.broadcasted_iota(jnp.int32, (blocks, toks), 0)
+    inside = (place >= 0) & (place < block_len)
+    alive = inside & (place.astype(jnp.float32) < column(len_ref[...].astype(jnp.float32)))
+    live = jnp.sum(jnp.where(alive, 1.0, 0.0), axis=0, keepdims=True)
+    per_token = jnp.sum(jnp.where(alive, block_weight, 0.0), axis=0, keepdims=True)
+    weight = combine_ref[...] * per_token
 
     rows8 = -(-ne // 8) * 8
     row_id = lax.broadcasted_iota(jnp.int32, (rows8, 1), 0)
@@ -77,10 +114,11 @@
     hit0 = routes_ref[0:1, :] == owner
     hit1 = routes_ref[1:2, :] == owner
     named = hit0 | hit1
-    tok_pos = ranks(named, toks)
-    tok_weight = jnp.where(hit0, weight_ref[0:1, :], 0.0) + jnp.where(hit1, weight_ref[1:2, :], 0.0)
+    tok_rank = ranks(named, toks)
+    tok_pos = tok_rank.astype(jnp.int32)
+    tok_weight = jnp.where(hit0, weight[0:1, :], 0.0) + jnp.where(hit1, weight[1:2, :], 0.0)
     in_order = (routes_ref[0:1, :] == row_id) | (routes_ref[1:2, :] == row_id)
-    counts = jnp.sum(jnp.where(in_order, live_ref[...], 0.0), axis=1, keepdims=True)
+    counts = jnp.sum(jnp.where(in_order, live, 0.0), axis=1, keepdims=True)
     lbuf[me] = jnp.broadcast_to(counts, (rows8, LANES))
 
     slot_tok = lax.broadcasted_iota(jnp.int32, (most, toks), 0)
@@ -156,12 +194,24 @@
     to_partners(m, me, e)
 
     slot_flat = lax.broadcasted_iota(jnp.int32, (most, 2 * toks), 0)
-    flat_pos = ranks(flat_ref[...] == owner, 2 * toks)
+    gap = lax.broadcasted_iota(jnp.int32, (toks, 2 * toks), 1) - 2 * lax.broadcasted_iota(
+        jnp.int32, (toks, 2 * toks), 0
+    )
+    flat_pos = -1.0
+    for k, hit in enumerate((hit0, hit1)):
+        spread = jnp.where(gap == k, 1.0, 0.0).astype(jnp.bfloat16)
+        value = jnp.where(hit, tok_rank + 1.0, 0.0)
+        high = jnp.floor(value * (1.0 / 16.0))
+        for part, unit in ((high, 16.0), (value - 16.0 * high, 1.0)):
+            flat_pos += unit * jnp.dot(part.astype(jnp.bfloat16), spread, preferred_element_type=jnp.float32)
+    flat_pos = flat_pos.astype(jnp.int32)
+    loads[-1].wait()
+    flat = (2 * toks, half)
+    h_rows = [h_in[:, :, c * half : (c + 1) * half].reshape(flat) for c in range(nd)]
     for j in [*range(1, ne), 0]:
         pick = jnp.where(slot_flat == flat_pos[j : j + 1, :], 1.0, 0.0).astype(jnp.bfloat16)
         for c in range(nd):
-            cols = pl.ds(c * half, half)
-            hs[j, c] = jnp.dot(pick, h_ref[:, cols], preferred_element_type=jnp.float32).astype(jnp.bfloat16)
+            hs[j, c] = jnp.dot(pick, h_rows[c], preferred_element_type=jnp.float32).astype(jnp.bfloat16)
         for i in range(nd):
             to = lax.rem(d + i, nd)
             if i or j:
@@ -266,7 +316,6 @@
 
 def fast_body(hidden, cotangent, routes, combine, block_pair, lengths, log_ratio):
     nd, ne, nm = lax.axis_size("dp"), lax.axis_size("expert"), lax.axis_size("mp")
-    per_token, within = token_factors(block_pair, lengths, log_ratio, LEN)
     toks, top, ff = hidden.shape
     width = cotangent.shape[1]
     most = 3 * toks // 4
@@ -277,9 +326,6 @@
     rows8 = -(-ne // 8) * 8
     dims = (nd, ne, nm, most, ca, cb)
     bf16, f32 = jnp.bfloat16, jnp.float32
-    routes_t = routes.T
-    weight_t = combine.T * per_token[None, :]
-    live = jnp.where(within, 1.0, 0.0).astype(f32)[None, :]
     vmem = pl.BlockSpec(memory_space=pltpu.VMEM)
     dma = pltpu.SemaphoreType.DMA
     hr, sa, sb, load = pl.pallas_call(
@@ -290,14 +336,22 @@
             jax.ShapeDtypeStruct((srcs, most, nm * cb), bf16),
             jax.ShapeDtypeStruct((rows8, LANES), f32),
         ),
-        in_specs=[vmem] * 6,
+        in_specs=[pl.BlockSpec(memory_space=pltpu.HBM)] * 7,
         out_specs=(vmem,) * 4,
         scratch_shapes=[
+            pltpu.VMEM((toks, top, ff), bf16),
+            pltpu.VMEM(cotangent.shape, bf16),
+            pltpu.VMEM((top, toks), jnp.int32),
+            pltpu.VMEM((top, toks), f32),
+            pltpu.VMEM(block_pair.shape, jnp.int32),
+            pltpu.VMEM(lengths.shape, jnp.int32),
+            pltpu.VMEM(log_ratio.shape, f32),
             pltpu.VMEM((ne, nd, most, half), bf16),
             pltpu.VMEM((ne, most, ca), bf16),
             pltpu.VMEM((ne, most, nm * cb), bf16),
             pltpu.VMEM((nm, toks, cb), bf16),
             pltpu.VMEM((srcs, rows8, LANES), f32),
+            dma((7,)),
             dma((ne,)),
             dma((nm, srcs)),
             dma((nm, ne)),
@@ -316,7 +370,7 @@
         compiler_params=pltpu.CompilerParams(
             collective_id=0, has_side_effects=True, vmem_limit_bytes=VMEM_ROOM
         ),
-    )(hidden.reshape(toks * top, ff), cotangent, routes_t, routes.reshape(1, toks * top), weight_t, live)
+    )(hidden, cotangent, routes.T, combine.T, block_pair, lengths, log_ratio)
     depth = srcs * most
     grad_down = pl.pallas_call(
         product_kernel,

time: 109 us -> 105 us (0.963)
  other arithmetic: 2.98 us -> 0 us
  local copies, waits for them, and re-layouts: 8.73 us -> 6.72 us
    reshape x2 -> x0, local copies, waits for them, and re-layouts: 5.87 us -> none  [the longest x1 5.71 us: fast_body(): hidden.reshape(toks * top, ff)]
    unnamed x5 -> x14, local copies, waits for them, and re-layouts: 0.82 us -> 6.1 us
    select_n x4 -> x0, other arithmetic: 1.36 us -> none  [the longest x1 0.68 us: token_factors(): owners = block_pair // 2]
where the time goes in v2:
time: 105 us; the launch traced here: 104 us
  Pallas kernels  97 us (92%)
  local copies, waits for them, and re-layouts  6.72 us (6%)
    pallas_call x1, Pallas kernels, fast_body(): pl.pallas_call(functools.partial(exchange_kernel, dims), out_shape=(jax.S...  82.4 us
    pallas_call x1, Pallas kernels, fast_body(): pl.pallas_call(product_kernel, out_shape=jax.ShapeDtypeStruct((1, half, n...  14.5 us
    unnamed x14, local copies, waits for them, and re-layouts  6.1 us

profile of v2, /device:TPU:0, one launch (start us, length us, event | category | flops | bytes accessed | tf_op | source)
XLA Modules:
  0.0 104.4 jit_solution(14246769536797696858)
XLA Ops:
  0.6 0.0 copy-start
  0.6 1.8 %copy-done = bf16[384,2,1792]{2,1,0:T(2,128)(2,1)S(1)} copy-done((bf16[384,2,1792]{2,1,0:T(2,128)(2,1)S(1)}, bf16[384,2,1792]{2,1,0:T(2,128)(2,1)}, u32[]{:S(2)}) %copy-start) | copy-done | bytes 2752536
  2.4 0.0 copy-start.1
  2.4 1.0 copy-done.1
  3.4 0.0 copy-start.2
  3.4 0.7 copy-done.2
  4.1 0.0 copy-start.3
  4.1 0.7 copy-done.3
  4.8 0.0 copy-start.4
  4.8 0.7 copy-done.4
  5.4 0.0 copy-start.5
  5.4 0.7 copy-done.5
  6.1 0.0 copy-start.6
  6.1 0.7 copy-done.6
  6.7 82.4 %shard_map.86 = (bf16[8,288,896]{2,1,0:T(8,128)(2,1)}, bf16[4,8,288,384]{3,2,1,0:T(8,128)(2,1)}, bf16[8,288,512]{2,1,0:T(8,128)(2,1)S(1)}, f32[8,128]{1,0:T(8,128)S(1)}) custom-call(bf16[384,2,1792]{2,1,0:T(2,128)(2,1)S(1)} %copy-done, bf16[384,512]{1,0:T(8,128)(2,1)S(1)} %copy-done.1, s32[2,384]{1,0:T(2,128)S(1)} %bitcast.6, f32[2,384]{1,0:T(2,128)S(1)} %bitcast.7, ...), custom_call_target="tpu_custom_call" | custom-call | tf_op jit(solution)/shard_map/pallas_call | solution.py:331
  89.2 14.5 %shard_map.87 = f32[1,896,2048]{2,1,0:T(8,128)} custom-call(bf16[2304,896]{1,0:T(8,128)(2,1)} %bitcast.9, bf16[4,2304,384]{2,1,0:T(8,128)(2,1)} %bitcast.8, bf16[2304,512]{1,0:T(8,128)(2,1)S(1)} %bitcast.5), custom_call_target="tpu_custom_call" | custom-call | tf_op jit(solution)/shard_map/pallas_call | solution.py:375
  103.7 0.6 slice_reduce_fusion
Async XLA Ops:
  0.6 1.8 %copy-start = (bf16[384,2,1792]{2,1,0:T(2,128)(2,1)S(1)}, bf16[384,2,1792]{2,1,0:T(2,128)(2,1)}, u32[]{:S(2)}) copy-start(bf16[384,2,1792]{2,1,0:T(2,128)(2,1)} %h_hbm.1) | copy-start | bytes 8257540
  2.4 1.0 copy-start.1
  3.4 0.7 copy-start.2
  4.1 0.7 copy-start.3
  4.8 0.7 copy-start.4
  5.4 0.7 copy-start.5
  6.1 0.7 copy-start.6

commit v3 on v2

--- a/solution.py
+++ b/solution.py
@@ -11,6 +11,7 @@
 LEN = 32
 LANES = 128
 VMEM_ROOM = 48 * 1024 * 1024
+VMEM_MOST = 67043328
 MESH = pl.DeviceIdType.MESH
 
 
@@ -37,9 +38,10 @@
 
 def exchange_kernel(
     dims, h_hbm, cot_hbm, routes_hbm, combine_hbm, pair_hbm, len_hbm, ratio_hbm,
-    hr, sa, sb, load_ref,
+    ht_out, acc_out, last_out, sb_out, load_ref,
     h_in, cot_ref, routes_ref, combine_ref, pair_ref, len_ref, ratio_ref,
-    hs, sas, sbs, cotb, lbuf, in_sem,
+    hr, sa, sb, ht, stage,
+    hs, sas, sbs, cotb, lbuf, in_sem, out_sem,
     xa_s, a_r, up_s, dn_s, dd_s, cb_s, cb_r, xb_s, b_r, db_s, h_s, h_r, l_s, l_r,
 ):
     nd, ne, nm, most, ca, cb = dims
@@ -119,7 +121,8 @@
     tok_weight = jnp.where(hit0, weight[0:1, :], 0.0) + jnp.where(hit1, weight[1:2, :], 0.0)
     in_order = (routes_ref[0:1, :] == row_id) | (routes_ref[1:2, :] == row_id)
     counts = jnp.sum(jnp.where(in_order, live, 0.0), axis=1, keepdims=True)
-    lbuf[me] = jnp.broadcast_to(counts, (rows8, LANES))
+    lanes8 = lax.broadcasted_iota(jnp.int32, (rows8, LANES), 1) == row_id
+    lbuf[me] = jnp.broadcast_to(jnp.sum(jnp.where(lanes8, counts, 0.0), axis=0, keepdims=True), (rows8, LANES))
 
     slot_tok = lax.broadcasted_iota(jnp.int32, (most, toks), 0)
     picks, scales = [], []
@@ -247,6 +250,41 @@
             copy.start()
             sends.append(copy)
 
+    depth = nd * ne * most
+    outs = []
+
+    def nearest(r):
+        near = jnp.minimum(m, nm - 1 - m)
+        both = m + (r + 1) // 2 * (1 if r % 2 == 0 else -1)
+        far = jnp.where(m < nm - 1 - m, m + r - near, m - r + near)
+        return jnp.where(r <= 2 * near, both, far)
+
+    def from_partners(q):
+        for i in range(1, nd):
+            for j in range(ne):
+                src = lax.rem(d + i, nd) * ne + j
+                wait_in(sa.at[q, src], a_r.at[q, src])
+
+    def send_out(src, dst):
+        copy = pltpu.make_async_copy(src, dst, out_sem.at[len(outs)])
+        copy.start()
+        outs.append(copy)
+
+    def all_hidden():
+        for i in range(nd):
+            for j in range(ne):
+                if i or j:
+                    src = lax.rem(d + i, nd) * ne + lax.rem(e + j, ne)
+                    wait_in(hr.at[src], h_r.at[src])
+        ht[...] = hr[...].reshape(depth, half).T
+        send_out(ht, ht_out)
+
+    def product(r):
+        q = nearest(r)
+        from_partners(q)
+        stage[r] = jnp.dot(ht[...], sa[q].reshape(depth, ca), preferred_element_type=jnp.float32)
+        send_out(stage.at[r], acc_out.at[q])
+
     for j in range(1, ne):
         ej = lax.rem(e + j, ne)
         src = d * ne + ej
@@ -256,8 +294,12 @@
     for k in range(1, nm):
         below, above = m - k, m + k
         ql, qh = lax.rem(below + nm, nm), lax.rem(above, nm)
-        never = m < 0
         for j in range(ne):
+            if k == nm - 1 and j % 2 == 0:
+                for r in range(j // 2 * (nm - 1) // 2, nm - 1 if j else (nm - 1) // 2):
+                    if r == 0:
+                        all_hidden()
+                    product(r)
             ej = lax.rem(e + j, ne)
             src = d * ne + ej
             wait_in(sa.at[ql, src], a_r.at[ql, src], below >= 0)
@@ -281,37 +323,54 @@
             copy.start()
             sends.append(copy)
 
+    last = nearest(nm - 1)
+    from_partners(last)
+    send_out(sa.at[last], last_out)
     for i in range(1, nd):
-        other = lax.rem(d + i, nd)
         for j in range(ne):
-            src = other * ne + j
+            src = lax.rem(d + i, nd) * ne + j
             wait_in(sb.at[src], b_r.at[src])
-            for q in range(nm):
-                wait_in(sa.at[q, src], a_r.at[q, src])
+    send_out(sb, sb_out)
     for i in range(nd):
         for j in range(ne):
             if i or j:
                 src = lax.rem(d + i, nd) * ne + lax.rem(e + j, ne)
-                wait_in(hr.at[src], h_r.at[src])
                 wait_in(lbuf.at[src], l_r.at[src])
     total = lbuf[0]
     for k in range(1, nd * ne):
         total = total + lbuf[k]
     load_ref[...] = total
 
+    for c in outs:
+        c.wait()
     for c in sends:
         c.wait_send()
     for go, c in guarded:
         pl.when(go)(c.wait_send)
 
 
-def product_kernel(h_ref, sa_ref, sb_ref, out_ref, turned):
-    @pl.when(pl.program_id(0) == 0)
+def product_kernel(ht_ref, acc_ref, last_ref, sb_ref, load_ref, out_ref, total_ref, dense):
+    q, nm = pl.program_id(0), pl.num_programs(0)
+    m = lax.axis_index("mp")
+    last = jnp.where(m < nm - 1 - m, nm - 1, 0)
+    ca, cb = acc_ref.shape[2], dense.shape[2]
+
+    @pl.when(q == 0)
     def _():
-        turned[...] = h_ref[...].T
-
-    rows = jnp.concatenate([sa_ref[0], sb_ref[...]], axis=1)
-    out_ref[0] = jnp.dot(turned[...], rows, preferred_element_type=jnp.float32)
+        total_ref[...] = load_ref[0:1, : total_ref.shape[1]]
+        cols = jnp.dot(ht_ref[...], sb_ref[...], preferred_element_type=jnp.float32)
+        for i in range(dense.shape[0]):
+            dense[i] = cols[:, i * cb : (i + 1) * cb]
+
+    @pl.when(q == last)
+    def _():
+        out_ref[0, :, :ca] = jnp.dot(ht_ref[...], last_ref[...], preferred_element_type=jnp.float32)
+
+    @pl.when(q != last)
+    def _():
+        out_ref[0, :, :ca] = acc_ref[0]
+
+    out_ref[0, :, ca:] = dense[q]
 
 
 def fast_body(hidden, cotangent, routes, combine, block_pair, lengths, log_ratio):
@@ -328,16 +387,18 @@
     bf16, f32 = jnp.bfloat16, jnp.float32
     vmem = pl.BlockSpec(memory_space=pltpu.VMEM)
     dma = pltpu.SemaphoreType.DMA
-    hr, sa, sb, load = pl.pallas_call(
+    depth = srcs * most
+    hidden_t, done, last, dense, load = pl.pallas_call(
         functools.partial(exchange_kernel, dims),
         out_shape=(
-            jax.ShapeDtypeStruct((srcs, most, half), bf16),
-            jax.ShapeDtypeStruct((nm, srcs, most, ca), bf16),
+            jax.ShapeDtypeStruct((half, depth), bf16),
+            jax.ShapeDtypeStruct((nm, half, ca), f32),
+            jax.ShapeDtypeStruct((srcs, most, ca), bf16),
             jax.ShapeDtypeStruct((srcs, most, nm * cb), bf16),
             jax.ShapeDtypeStruct((rows8, LANES), f32),
         ),
         in_specs=[pl.BlockSpec(memory_space=pltpu.HBM)] * 7,
-        out_specs=(vmem,) * 4,
+        out_specs=(pl.BlockSpec(memory_space=pltpu.HBM),) * 4 + (vmem,),
         scratch_shapes=[
             pltpu.VMEM((toks, top, ff), bf16),
             pltpu.VMEM(cotangent.shape, bf16),
@@ -346,12 +407,18 @@
             pltpu.VMEM(block_pair.shape, jnp.int32),
             pltpu.VMEM(lengths.shape, jnp.int32),
             pltpu.VMEM(log_ratio.shape, f32),
+            pltpu.VMEM((srcs, most, half), bf16),
+            pltpu.VMEM((nm, srcs, most, ca), bf16),
+            pltpu.VMEM((srcs, most, nm * cb), bf16),
+            pltpu.VMEM((half, depth), bf16),
+            pltpu.VMEM((nm - 1, half, ca), f32),
             pltpu.VMEM((ne, nd, most, half), bf16),
             pltpu.VMEM((ne, most, ca), bf16),
             pltpu.VMEM((ne, most, nm * cb), bf16),
             pltpu.VMEM((nm, toks, cb), bf16),
             pltpu.VMEM((srcs, rows8, LANES), f32),
             dma((7,)),
+            dma((nm + 2,)),
             dma((ne,)),
             dma((nm, srcs)),
             dma((nm, ne)),
@@ -368,24 +435,28 @@
             dma((srcs,)),
         ],
         compiler_params=pltpu.CompilerParams(
-            collective_id=0, has_side_effects=True, vmem_limit_bytes=VMEM_ROOM
+            collective_id=0, has_side_effects=True, vmem_limit_bytes=VMEM_MOST
         ),
     )(hidden, cotangent, routes.T, combine.T, block_pair, lengths, log_ratio)
-    depth = srcs * most
-    grad_down = pl.pallas_call(
+    grad_down, total = pl.pallas_call(
         product_kernel,
-        out_shape=jax.ShapeDtypeStruct((1, half, nm * width), f32),
+        out_shape=(jax.ShapeDtypeStruct((1, half, nm * width), f32), jax.ShapeDtypeStruct((1, ne), f32)),
         grid=(nm,),
         in_specs=[
-            pl.BlockSpec((depth, half), lambda q: (0, 0)),
-            pl.BlockSpec((1, depth, ca), lambda q: (q, 0, 0)),
-            pl.BlockSpec((depth, cb), lambda q: (0, q)),
+            pl.BlockSpec((half, depth), lambda q: (0, 0)),
+            pl.BlockSpec((1, half, ca), lambda q: (q, 0, 0)),
+            pl.BlockSpec((depth, ca), lambda q: (0, 0)),
+            pl.BlockSpec((depth, nm * cb), lambda q: (0, 0)),
+            pl.BlockSpec((rows8, LANES), lambda q: (0, 0)),
         ],
-        out_specs=pl.BlockSpec((1, half, width), lambda q: (0, 0, q)),
-        scratch_shapes=[pltpu.VMEM((half, depth), bf16)],
-        compiler_params=pltpu.CompilerParams(vmem_limit_bytes=VMEM_ROOM),
-    )(hr.reshape(depth, half), sa.reshape(nm, depth, ca), sb.reshape(depth, nm * cb))
-    return grad_down, load[:ne, 0]
+        out_specs=(
+            pl.BlockSpec((1, half, width), lambda q: (0, 0, q)),
+            pl.BlockSpec((1, ne), lambda q: (0, 0)),
+        ),
+        scratch_shapes=[pltpu.VMEM((nm, half, cb), f32)],
+        compiler_params=pltpu.CompilerParams(vmem_limit_bytes=VMEM_MOST),
+    )(hidden_t, done, last.reshape(depth, ca), dense.reshape(depth, nm * cb), load)
+    return grad_down, total.reshape(ne)
 
 
 def plain_body(hidden, cotangent, routes, combine, block_pair, lengths, log_ratio):

time: 105 us -> 93.6 us (0.89)
  local copies, waits for them, and re-layouts: 6.72 us -> 0 us
  Pallas kernels: 97 us -> 91.8 us
    unnamed x14 -> x0, local copies, waits for them, and re-layouts: 6.1 us -> none
    pallas_call x1, Pallas kernels: 82.4 us -> 78.8 us  [fast_body(): pl.pallas_call(functools.partial(exchange_kernel, dims), out_shape=(jax.S...]
    pallas_call x1, Pallas kernels: 14.5 us -> 13 us  [fast_body(): pl.pallas_call(product_kernel, out_shape=(jax.ShapeDtypeStruct((1, half,...]
where the time goes in v3:
time: 93.6 us; the launch traced here: 92.4 us
  Pallas kernels  91.8 us (98%)
    pallas_call x1, Pallas kernels, fast_body(): pl.pallas_call(functools.partial(exchange_kernel, dims), out_shape=(jax.S...  78.8 us
    pallas_call x1, Pallas kernels, fast_body(): pl.pallas_call(product_kernel, out_shape=(jax.ShapeDtypeStruct((1, half,...  13 us

profile of v3, /device:TPU:0, one launch (start us, length us, event | category | flops | bytes accessed | tf_op | source)
XLA Modules:
  0.0 92.4 jit_solution(9624302864820748532)
XLA Ops:
  0.6 78.8 %shard_map.86 = (bf16[896,2304]{1,0:T(8,128)(2,1)}, f32[4,896,384]{2,1,0:T(8,128)}, bf16[8,288,384]{2,1,0:T(8,128)(2,1)}, bf16[8,288,512]{2,1,0:T(8,128)(2,1)}, f32[8,128]{1,0:T(8,128)}) custom-call(bf16[384,2,1792]{2,1,0:T(2,128)(2,1)} %h_hbm.1, bf16[384,512]{1,0:T(8,128)(2,1)} %cot_hbm.1, s32[2,384]{1,0:T(2,128)} %bitcast.7, f32[2,384]{1,0:T(2,128)} %bitcast.8, ...), custom_call_target="tpu_custom_call" | custom-call | tf_op jit(solution)/shard_map/pallas_call | solution.py:391
  79.4 13.0 %shard_map.87 = (f32[1,896,2048]{2,1,0:T(8,128)}, f32[1,4]{1,0:T(1,128)}) custom-call(bf16[896,2304]{1,0:T(8,128)(2,1)} %get-tuple-element.9.ht_ref, f32[4,896,384]{2,1,0:T(8,128)} %get-tuple-element.10.acc_ref, bf16[2304,384]{1,0:T(8,128)(2,1)} %bitcast.6, bf16[2304,512]{1,0:T(8,128)(2,1)} %bitcast.5, f32[8,128]{1,0:T(8,128)} %get-tuple-element.13.load_ref), custom_call_target="tpu_custom_call" | custom-call | tf_op jit(solution)/shard_map/pallas_call | solution.py:441

commit v4 on v3

--- a/solution.py
+++ b/solution.py
@@ -349,28 +349,17 @@
         pl.when(go)(c.wait_send)
 
 
-def product_kernel(ht_ref, acc_ref, last_ref, sb_ref, load_ref, out_ref, total_ref, dense):
-    q, nm = pl.program_id(0), pl.num_programs(0)
+def product_kernel(nm, ht_ref, acc_ref, last_ref, sb_ref, load_ref, out_ref, total_ref):
     m = lax.axis_index("mp")
     last = jnp.where(m < nm - 1 - m, nm - 1, 0)
-    ca, cb = acc_ref.shape[2], dense.shape[2]
-
-    @pl.when(q == 0)
-    def _():
-        total_ref[...] = load_ref[0:1, : total_ref.shape[1]]
-        cols = jnp.dot(ht_ref[...], sb_ref[...], preferred_element_type=jnp.float32)
-        for i in range(dense.shape[0]):
-            dense[i] = cols[:, i * cb : (i + 1) * cb]
-
-    @pl.when(q == last)
-    def _():
-        out_ref[0, :, :ca] = jnp.dot(ht_ref[...], last_ref[...], preferred_element_type=jnp.float32)
-
-    @pl.when(q != last)
-    def _():
-        out_ref[0, :, :ca] = acc_ref[0]
-
-    out_ref[0, :, ca:] = dense[q]
+    ca, cb = acc_ref.shape[2], sb_ref.shape[1] // nm
+    width = ca + cb
+    total_ref[...] = load_ref[0:1, : total_ref.shape[1]]
+    tail = jnp.dot(ht_ref[...], last_ref[...], preferred_element_type=jnp.float32)
+    cols = jnp.dot(ht_ref[...], sb_ref[...], preferred_element_type=jnp.float32)
+    for q in range(nm):
+        out_ref[0, :, q * width + ca : (q + 1) * width] = cols[:, q * cb : (q + 1) * cb]
+        out_ref[0, :, q * width : q * width + ca] = jnp.where(last == q, tail, acc_ref[q])
 
 
 def fast_body(hidden, cotangent, routes, combine, block_pair, lengths, log_ratio):
@@ -438,22 +427,23 @@
             collective_id=0, has_side_effects=True, vmem_limit_bytes=VMEM_MOST
         ),
     )(hidden, cotangent, routes.T, combine.T, block_pair, lengths, log_ratio)
+    steps = next(n for n in (4, 2, 1) if half % (16 * n) == 0 or n == 1)
+    rows = half // steps
     grad_down, total = pl.pallas_call(
-        product_kernel,
+        functools.partial(product_kernel, nm),
         out_shape=(jax.ShapeDtypeStruct((1, half, nm * width), f32), jax.ShapeDtypeStruct((1, ne), f32)),
-        grid=(nm,),
+        grid=(steps,),
         in_specs=[
-            pl.BlockSpec((half, depth), lambda q: (0, 0)),
-            pl.BlockSpec((1, half, ca), lambda q: (q, 0, 0)),
-            pl.BlockSpec((depth, ca), lambda q: (0, 0)),
-            pl.BlockSpec((depth, nm * cb), lambda q: (0, 0)),
-            pl.BlockSpec((rows8, LANES), lambda q: (0, 0)),
+            pl.BlockSpec((rows, depth), lambda i: (i, 0)),
+            pl.BlockSpec((nm, rows, ca), lambda i: (0, i, 0)),
+            pl.BlockSpec((depth, ca), lambda i: (0, 0)),
+            pl.BlockSpec((depth, nm * cb), lambda i: (0, 0)),
+            pl.BlockSpec((rows8, LANES), lambda i: (0, 0)),
         ],
         out_specs=(
-            pl.BlockSpec((1, half, width), lambda q: (0, 0, q)),
-            pl.BlockSpec((1, ne), lambda q: (0, 0)),
+            pl.BlockSpec((1, rows, nm * width), lambda i: (0, i, 0)),
+            pl.BlockSpec((1, ne), lambda i: (0, 0)),
         ),
-        scratch_shapes=[pltpu.VMEM((nm, half, cb), f32)],
         compiler_params=pltpu.CompilerParams(vmem_limit_bytes=VMEM_MOST),
     )(hidden_t, done, last.reshape(depth, ca), dense.reshape(depth, nm * cb), load)
     return grad_down, total.reshape(ne)

time: 93.6 us -> 91.2 us (0.974)
  Pallas kernels: 91.8 us -> 89.3 us
    pallas_call x1, Pallas kernels: 13 us -> 10.6 us  [fast_body(): pl.pallas_call(functools.partial(product_kernel, nm), out_shape=(jax.Shap...]
where the time goes in v4:
time: 91.2 us; the launch traced here: 90 us
  Pallas kernels  89.3 us (98%)
    pallas_call x1, Pallas kernels, fast_body(): pl.pallas_call(functools.partial(exchange_kernel, dims), out_shape=(jax.S...  78.8 us
    pallas_call x1, Pallas kernels, fast_body(): pl.pallas_call(functools.partial(product_kernel, nm), out_shape=(jax.Shap...  10.6 us

profile of v4, /device:TPU:0, one launch (start us, length us, event | category | flops | bytes accessed | tf_op | source)
XLA Modules:
  0.0 90.0 jit_solution(3660655650415910480)
XLA Ops:
  0.6 78.8 %shard_map.86 = (bf16[896,2304]{1,0:T(8,128)(2,1)}, f32[4,896,384]{2,1,0:T(8,128)}, bf16[8,288,384]{2,1,0:T(8,128)(2,1)}, bf16[8,288,512]{2,1,0:T(8,128)(2,1)}, f32[8,128]{1,0:T(8,128)}) custom-call(bf16[384,2,1792]{2,1,0:T(2,128)(2,1)} %h_hbm.1, bf16[384,512]{1,0:T(8,128)(2,1)} %cot_hbm.1, s32[2,384]{1,0:T(2,128)} %bitcast.7, f32[2,384]{1,0:T(2,128)} %bitcast.8, ...), custom_call_target="tpu_custom_call" | custom-call | tf_op jit(solution)/shard_map/pallas_call | solution.py:380
  79.4 10.6 %shard_map.87 = (f32[1,896,2048]{2,1,0:T(8,128)}, f32[1,4]{1,0:T(1,128)}) custom-call(bf16[896,2304]{1,0:T(8,128)(2,1)} %get-tuple-element.9.ht_ref, f32[4,896,384]{2,1,0:T(8,128)} %get-tuple-element.10.acc_ref, bf16[2304,384]{1,0:T(8,128)(2,1)} %bitcast.6, bf16[2304,512]{1,0:T(8,128)(2,1)} %bitcast.5, f32[8,128]{1,0:T(8,128)} %get-tuple-element.13.load_ref), custom_call_target="tpu_custom_call" | custom-call | tf_op jit(solution)/shard_map/pallas_call | solution.py:432
